TPU v7x, 32 devices: a whole 2x2x4 slice. The times are simulated.
32 devices in a mesh: seq: 16 (over z, x, core), head: 2 (over y).
Axes of the slice: x: 2, y: 2, z: 4, core: 2. Of those that a mesh axis runs over, the one named last changes fastest.
Arguments:
- hidden: bfloat16 [4608, 8192], P('seq'), may hold values from -6 to 6
- norm_gain: bfloat16 [8192], replicated, may hold values from 0.099609375 to 1.8984375
- w_query: bfloat16 [8192, 1024], P('seq', 'head'), may hold values from -0.125 to 0.125
- w_key: bfloat16 [8192, 256], P('seq', 'head'), may hold values from -0.125 to 0.125
- w_value: bfloat16 [8192, 256], P('seq', 'head'), may hold values from -0.0625 to 0.0625
- bias_query: bfloat16 [1024], P('head'), may hold values from -3 to 3
- bias_key: bfloat16 [256], P('head'), may hold values from -200 to 200
- bias_value: bfloat16 [256], P('head'), may hold values from -3 to 3
- w_out: bfloat16 [1024, 8192], P('head', 'seq'), may hold values from -0.1875 to 0.1875
Outputs:
- attn_out: bfloat16 [4608, 8192], P(('seq', 'head'))
All inputs are finite; a program needn't handle non-finite values.
Results may differ from a plain program's by a relative error of at most 0.014.
The roundings to bfloat16 on the way count: a program that leaves them out, or rounds other values in their place, can miss the bound.
Values may be sent and summed in bfloat16 or wider, within the bound.
No kernel may reach another device: no remote copies, remote signals or barrier semaphores. Data moves between devices by JAX's collectives and lax.ppermute only.
A program may use at most 192 MiB of HBM per device.

v0:
```python
import jax
import jax.numpy as jnp
from jax import lax
from jax.sharding import PartitionSpec as P

HEAD_DIM = 128
ROPE_BASE = 1000000.0
EPSILON = 1e-06


def rotary(values, positions):
    half_dim = values.shape[-1] // 2
    freq = ROPE_BASE ** (-2.0 * jnp.arange(half_dim, dtype=jnp.float32) / values.shape[-1])
    angles = positions.astype(jnp.float32)[:, None, None] * freq[None, None, :]
    cosine = jnp.cos(angles)
    sine = jnp.sin(angles)
    first = values[..., :half_dim]
    second = values[..., half_dim:]
    return jnp.concatenate(
        [first * cosine - second * sine, second * cosine + first * sine], axis=-1
    )


def local(hidden, norm_gain, w_query, w_key, w_value, bias_query, bias_key, bias_value, w_out):
    row_count = hidden.shape[0]
    head_count = w_query.shape[1] // HEAD_DIM
    first_row = lax.axis_index("seq") * row_count
    last_row = first_row + row_count - 1
    positions = first_row + jnp.arange(row_count, dtype=jnp.int32)
    widened = hidden.astype(jnp.float32)
    inverse = lax.rsqrt(jnp.mean(widened * widened, axis=-1, keepdims=True) + EPSILON)
    normed = (widened * inverse * norm_gain.astype(jnp.float32)).astype(jnp.bfloat16)
    query = jnp.dot(
        normed,
        lax.all_gather(w_query, "seq", axis=0, tiled=True),
        preferred_element_type=jnp.float32,
    )
    keys = jnp.dot(
        normed, lax.all_gather(w_key, "seq", axis=0, tiled=True), preferred_element_type=jnp.float32
    )
    values = jnp.dot(
        normed,
        lax.all_gather(w_value, "seq", axis=0, tiled=True),
        preferred_element_type=jnp.float32,
    )
    query = query + bias_query.astype(jnp.float32)
    keys = keys + bias_key.astype(jnp.float32)
    values = values + bias_value.astype(jnp.float32)
    query = rotary(query.reshape(row_count, head_count, HEAD_DIM), positions).astype(jnp.bfloat16)
    keys = (
        rotary(keys.reshape(row_count, 1, HEAD_DIM), positions)
        .reshape(row_count, HEAD_DIM)
        .astype(jnp.bfloat16)
    )
    values = values.astype(jnp.bfloat16)
    query_heads = query.transpose(1, 0, 2)
    scaling = HEAD_DIM ** (-0.5)
    initial = (
        jnp.full((head_count, row_count), -1e30, jnp.float32),
        jnp.zeros((head_count, row_count), jnp.float32),
        jnp.zeros((head_count, row_count, HEAD_DIM), jnp.float32),
    )
    key_piece = lax.all_gather(keys, "seq", axis=0, tiled=True)
    value_piece = lax.all_gather(values, "seq", axis=0, tiled=True)

    def update(state):
        highest, total, summed = state
        scores = (
            jnp.einsum("hqd,kd->hqk", query_heads, key_piece, preferred_element_type=jnp.float32)
            * scaling
        )
        key_positions = jnp.arange(key_piece.shape[0], dtype=jnp.int32)
        allowed = positions[:, None] >= key_positions[None, :]
        scores = jnp.where(allowed[None], scores, -jnp.inf)
        new_high = jnp.maximum(highest, jnp.max(scores, axis=-1))
        probs = jnp.exp(scores - new_high[..., None])
        total = jnp.sum(probs, axis=-1)
        mixed = jnp.einsum(
            "hqk,kd->hqd",
            probs.astype(jnp.bfloat16),
            value_piece,
            preferred_element_type=jnp.float32,
        )
        return (new_high, total, mixed)

    def unchanged(state):
        return state

    highest, total, summed = lax.cond(jnp.int32(0) <= last_row, update, unchanged, initial)
    attended = (summed / total[..., None]).astype(jnp.bfloat16)
    attended = attended.transpose(1, 0, 2).reshape(row_count, head_count * HEAD_DIM)
    partial_out = jnp.dot(
        attended,
        lax.all_gather(w_out, "seq", axis=1, tiled=True),
        preferred_element_type=jnp.float32,
    )
    result = lax.psum_scatter(
        partial_out.astype(jnp.bfloat16), "head", scatter_dimension=0, tiled=True
    )
    return result


def solution(mesh):
    in_specs = (
        P("seq", None),
        P(),
        P("seq", "head"),
        P("seq", "head"),
        P("seq", "head"),
        P("head"),
        P("head"),
        P("head"),
        P("head", "seq"),
    )
    out_specs = P(("seq", "head"), None)
    return jax.shard_map(local, mesh=mesh, in_specs=in_specs, out_specs=out_specs, check_vma=False)
```

profile of v0, /device:TPU:0, one launch (start us, length us, event | category | flops | bytes accessed | tf_op | source)
XLA Modules:
  0.0 401.3 jit_solution(17232137514900571910)
XLA Ops:
  6.5 0.7 all-gather.10.cloned.1.call-update
  7.3 0.7 all-gather.12.cloned.1.call-update
  8.1 0.7 all-gather.8.cloned.1.call-update
  8.8 0.7 convert_element_type.48
  9.5 0.7 convert_element_type.52
  10.2 3.4 fusion.11
  13.6 40.1 %all-gather.10.cloned.1.call-done = bf16[8192,128]{1,0:T(8,128)(2,1)} async-done(((bf16[512,128]{1,0:T(8,128)(2,1)}), bf16[8192,128]{1,0:T(8,128)(2,1)}) %all-gather.10.cloned.1.call-update) | async-done | bytes 2097168 | tf_op jit(solution)/shard_map/all_gather | solution.py:39
  53.7 4.6 %fusion.14 = f32[288,1,128]{2,0,1:T(8,128)S(1)} fusion(bf16[8192,128]{1,0:T(8,128)(2,1)} %all-gather.10.cloned.1.call-done, f32[128]{0:T(128)S(1)} %convert_element_type.52, bf16[288,8192]{1,0:T(8,128)(2,1)} %param.11, f32[8192]{0:T(1024)S(1)} %convert_element_type.48, f32[288]{0:T(512)S(1)} %add_rsqrt_fusion), kind=kOutput, calls=%fused_computation.24 | convolution fusion | flops 613453824 | bytes 6997632 | tf_op jit(solution)/shard_map/dot_general | solution.py:38
  58.3 0.7 fusion.24
  58.9 0.7 pad_maximum_fusion
  59.8 36.3 %all-gather.12.cloned.1.call-done = bf16[8192,128]{1,0:T(8,128)(2,1)} async-done(((bf16[512,128]{1,0:T(8,128)(2,1)}), bf16[8192,128]{1,0:T(8,128)(2,1)}) %all-gather.12.cloned.1.call-update) | async-done | bytes 2097168 | tf_op jit(solution)/shard_map/all_gather | solution.py:43
  96.1 5.1 %fusion.15 = bf16[288,128]{1,0:T(8,128)(2,1)} fusion(bf16[8192,128]{1,0:T(8,128)(2,1)} %all-gather.12.cloned.1.call-done, f32[128]{0:T(128)S(1)} %convert_element_type.54, bf16[288,8192]{1,0:T(8,128)(2,1)} %param.11, f32[8192]{0:T(1024)S(1)} %convert_element_type.48, f32[288]{0:T(512)S(1)} %add_rsqrt_fusion), kind=kOutput, calls=%fused_computation.25 | convolution fusion | flops 613490688 | bytes 6923904 | tf_op jit(solution)/shard_map/dot_general | solution.py:41
  102.7 68.6 %all-gather.8.cloned.1.call-done = bf16[8192,512]{1,0:T(8,128)(2,1)} async-done(((bf16[512,512]{1,0:T(8,128)(2,1)}), bf16[8192,512]{1,0:T(8,128)(2,1)}) %all-gather.8.cloned.1.call-update) | async-done | bytes 8388624 | tf_op jit(solution)/shard_map/all_gather | solution.py:35
  171.3 7.0 %convolution_add_fusion = f32[288,512]{1,0:T(8,128)S(1)} fusion(bf16[8192,512]{1,0:T(8,128)(2,1)} %all-gather.8.cloned.1.call-done, f32[512]{0:T(512)S(1)} %convert_element_type.50, bf16[288,8192]{1,0:T(8,128)(2,1)} %param.11, f32[8192]{0:T(1024)S(1)} %convert_element_type.48, f32[288]{0:T(512)S(1)} %add_rsqrt_fusion), kind=kOutput, calls=%fused_computation.21 | convolution fusion | flops 2425503744 | bytes 13732992 | tf_op jit(solution)/shard_map/dot_general | solution.py:33
  179.3 31.1 %all-gather.18.cloned.1.call-done = bf16[4608,1,128]{2,0,1:T(8,128)(2,1)} async-done(((bf16[288,1,128]{2,0,1:T(8,128)(2,1)}), bf16[4608,1,128]{2,0,1:T(8,128)(2,1)}) %all-gather.18.cloned.1.call-update) | async-done | bytes 1179664 | tf_op jit(solution)/shard_map/all_gather | solution.py:63
  210.3 39.3 %all-gather.14.cloned.1.call-done = bf16[4608,128]{1,0:T(8,128)(2,1)} async-done(((bf16[288,128]{1,0:T(8,128)(2,1)}), bf16[4608,128]{1,0:T(8,128)(2,1)}) %all-gather.14.cloned.1.call-update) | async-done | bytes 1179664 | tf_op jit(solution)/shard_map/all_gather | solution.py:64
  249.7 19.5 %conditional.1 = (f32[4,288]{1,0:T(4,128)S(1)}, f32[4,288,128]{2,1,0:T(8,128)S(1)}) conditional(s32[]{:T(128)} %convert_element_type.46, () %tuple.13, (s32[]{:T(128)}, s32[288]{0:T(512)S(1)}, bf16[4,288,128]{2,1,0:T(8,128)(2,1)S(1)}, bf16[4608,128]{1,0:T(8,128)(2,1)}, bf16[4608,128]{1,0:T(8,128)(2,1)}) %tuple.36), branch_computations={%region_1.0_spmd, %region_2.5_spmd} | conditional | flops 2777627648 | bytes 72284560 | solution.py:89
  249.7 0.8 iota_compare_fusion
  250.5 5.5 %fusion = (f32[4,288]{1,0:T(4,128)S(1)}, f32[4,288,4608]{2,1,0:T(8,128)S(1)}) fusion(pred[288,4608]{1,0:T(8,128)(4,1)S(1)} %iota_compare_fusion, bf16[4,288,128]{2,1,0:T(8,128)(2,1)S(1)} %get-tuple-element.19, bf16[4608,128]{1,0:T(8,128)(2,1)} %get-tuple-element.20), kind=kOutput, calls=%fused_computation.2 | convolution fusion | flops 1374878592 | bytes 24039936 | tf_op jit(solution)/shard_map/cond/branch_1_fun/hqd,kd->hqk/dot_general | solution.py:69
  255.9 6.6 %fusion.3 = f32[4,288,128]{2,1,0:T(8,128)S(1)} fusion(f32[4,288,4608]{2,1,0:T(8,128)S(1)} %get-tuple-element.27, f32[4,288]{1,0:T(4,128)S(1)} %broadcast_maximum_fusion, pred[288,4608]{1,0:T(8,128)(4,1)S(1)} %iota_compare_fusion, bf16[4608,128]{1,0:T(8,128)(2,1)} %get-tuple-element.21), kind=kOutput, calls=%fused_computation.5 | convolution fusion | flops 1380188160 | bytes 24334848 | tf_op jit(solution)/shard_map/cond/branch_1_fun/hqk,kd->hqd/dot_general | solution.py:78
  262.6 6.6 %fusion.2 = f32[4,288]{1,0:T(4,128)S(1)} fusion(f32[4,288,4608]{2,1,0:T(8,128)S(1)} %get-tuple-element.27, f32[4,288]{1,0:T(4,128)S(1)} %broadcast_maximum_fusion, pred[288,4608]{1,0:T(8,128)(4,1)S(1)} %iota_compare_fusion), kind=kLoop, calls=%fused_computation.4 | loop fusion | flops 21232512 | bytes 22569984 | tf_op jit(solution)/shard_map/cond/branch_1_fun/reduce_sum | solution.py:77
  269.2 59.2 %all-gather.16.cloned.1.call-done = bf16[512,8192]{1,0:T(8,128)(2,1)} async-done(((bf16[512,512]{1,0:T(8,128)(2,1)}), bf16[512,8192]{1,0:T(8,128)(2,1)}) %all-gather.16.cloned.1.call-update) | async-done | bytes 8388624 | tf_op jit(solution)/shard_map/all_gather | solution.py:94
  328.3 7.7 %convolution_convert_fusion = bf16[288,8192]{1,0:T(8,128)(2,1)} fusion(bf16[512,8192]{1,0:T(8,128)(2,1)} %all-gather.16.cloned.1.call-done, f32[4,288,128]{2,1,0:T(8,128)S(1)} %get-tuple-element.24, f32[4,288]{1,0:T(4,128)S(1)} %get-tuple-element.25), kind=kOutput, calls=%fused_computation.17 | convolution fusion | flops 2418573312 | bytes 13701632 | tf_op jit(solution)/shard_map/dot_general | solution.py:92
  336.1 58.4 %reduce-scatter.2.cloned.1.call-done = bf16[144,8192]{1,0:T(8,128)(2,1)} async-done(((bf16[288,8192]{1,0:T(8,128)(2,1)}), bf16[144,8192]{1,0:T(8,128)(2,1)}) %reduce-scatter.2.cloned.1.call-update) | async-done | bytes 2359312 | tf_op jit(solution)/shard_map/reduce_scatter | solution.py:97
  (28 shorter events, 2.5 us)
Async XLA Ops:
  6.5 47.2 %all-gather.10.cloned.1.call-start = ((), (), s32[]{:S(2)}) async-start(), calls=%async_computation.2 | async-start | bytes 2228224 | tf_op jit(solution)/shard_map/all_gather | solution.py:39
  7.3 88.8 %all-gather.12.cloned.1.call-start = ((), (), s32[]{:S(2)}) async-start(), calls=%async_computation.3 | async-start | bytes 2228224 | tf_op jit(solution)/shard_map/all_gather | solution.py:43
  8.0 163.3 %all-gather.8.cloned.1.call-start = ((), (), s32[]{:S(2)}) async-start(), calls=%async_computation.1 | async-start | bytes 8912896 | tf_op jit(solution)/shard_map/all_gather | solution.py:35
  8.7 201.6 %all-gather.18.cloned.1.call-start = ((), (), s32[]{:S(2)}) async-start(), calls=%async_computation.7 | async-start | bytes 1253376 | tf_op jit(solution)/shard_map/all_gather | solution.py:63
  13.5 46.2 %copy-start.1 = (bf16[128]{0:T(256)(128)(2,1)S(1)}, bf16[128]{0:T(256)(128)(2,1)}, u32[]{:S(2)}) copy-start(bf16[128]{0:T(256)(128)(2,1)} %param.18) | copy-start | bytes 772
  58.3 43.8 %copy-start = (bf16[512]{0:T(512)(128)(2,1)S(1)}, bf16[512]{0:T(512)(128)(2,1)}, u32[]{:S(2)}) copy-start(bf16[512]{0:T(512)(128)(2,1)} %param.16) | copy-start | bytes 3076
  59.7 190.0 %all-gather.14.cloned.1.call-start = ((), (), s32[]{:S(2)}) async-start(), calls=%async_computation.4 | async-start | bytes 1253376 | tf_op jit(solution)/shard_map/all_gather | solution.py:64
  101.2 227.1 %all-gather.16.cloned.1.call-start = ((), (), s32[]{:S(2)}) async-start(), calls=%async_computation.5 | async-start | bytes 8912896 | tf_op jit(solution)/shard_map/all_gather | solution.py:94
  101.8 292.6 %reduce-scatter.2.cloned.1.call-start = ((), (), s32[]{:S(2)}) async-start(), calls=%async_computation.6 | async-start | bytes 7077888 | tf_op jit(solution)/shard_map/reduce_scatter | solution.py:97
Sparse Core Ops, SparseCore 0:
  9.5 44.1 all-gather.9
  55.9 40.1 all-gather.11
  98.2 73.0 all-gather.7
  173.4 36.8 all-gather.17
  212.5 37.1 all-gather.13
  251.7 76.5 all-gather.15
  336.2 58.2 reduce-scatter.1
where the time goes:
time: 402 us; the launch traced here: 401 us
  waiting for transfers between devices  336 us (84%)
  matrix products  36.6 us (9%)
  other arithmetic  14.4 us (4%)
  between operations  13.6 us (3%)
    all_gather x1, waiting for transfers between devices, local(): lax.all_gather(w_query, 'seq', axis=0, tiled=True)  68.6 us
    all_gather x1, waiting for transfers between devices, local(): lax.all_gather(w_out, 'seq', axis=1, tiled=True)  59.2 us
    reduce_scatter x1, waiting for transfers between devices, local(): lax.psum_scatter(partial_out.astype(jnp.bfloat16), 'head', scatter_dimens...  58.4 us
    all_gather x1, waiting for transfers between devices, local(): lax.all_gather(w_key, 'seq', axis=0, tiled=True)  40.1 us
    all_gather x1, waiting for transfers between devices, local(): value_piece = lax.all_gather(values, 'seq', axis=0, tiled=True)  39.3 us
    all_gather x1, waiting for transfers between devices, local(): lax.all_gather(w_value, 'seq', axis=0, tiled=True)  36.3 us
    all_gather x1, waiting for transfers between devices, local(): key_piece = lax.all_gather(keys, 'seq', axis=0, tiled=True)  31.1 us
  transfers between devices with their start and end apart: 7, of which 7 were waited for; matrix products, arithmetic and copies ran while one was open for 11% of the time, Pallas kernels for 0%

commit v1 on v0

--- a/solution.py
+++ b/solution.py
@@ -6,6 +6,32 @@
 HEAD_DIM = 128
 ROPE_BASE = 1000000.0
 EPSILON = 1e-06
+
+
+def recover_the_indices(shard_in, along_axis="seq"):
+    axis_n = lax.axis_size(along_axis)
+    line_up = []
+    no = 0
+    while no < axis_n:
+        line_up.append((no, (no + 1) % axis_n))
+        no = no + 1
+    arrivals = []
+    no = 0
+    while no < axis_n:
+        arrivals.append((no, (no - 1) % axis_n))
+        no += 1
+    mid_arr, w1 = ([shard_in], [shard_in])
+    for _ in range(axis_n // 2):
+        base_arr = lax.ppermute(mid_arr[-1], along_axis, line_up)
+        mid_arr.append(base_arr)
+    rr = 0
+    while rr < (axis_n - 1) // 2:
+        n_now = lax.ppermute(w1[-1], axis_name=along_axis, perm=arrivals)
+        w1.append(n_now)
+        rr = rr + 1
+    fresh = jnp.concatenate([*mid_arr[::-1], *w1[1:]], axis=0)
+    later = lax.axis_index(along_axis)
+    return jnp.roll(fresh, (later - axis_n // 2) * shard_in.shape[0], axis=0)
 
 
 def rotary(values, positions):
@@ -60,7 +86,7 @@
         jnp.zeros((head_count, row_count), jnp.float32),
         jnp.zeros((head_count, row_count, HEAD_DIM), jnp.float32),
     )
-    key_piece = lax.all_gather(keys, "seq", axis=0, tiled=True)
+    key_piece = recover_the_indices(keys)
     value_piece = lax.all_gather(values, "seq", axis=0, tiled=True)
 
     def update(state):

time: 402 us -> 369 us (0.918)
  waiting for transfers between devices: 336 us -> 252 us
  starting transfers between devices: 0.42 us -> 32.2 us
  local copies, waits for them, and re-layouts: 0.59 us -> 21 us
    all_gather x1, waiting for transfers between devices: 68.6 us -> 0.01 us  [local(): lax.all_gather(w_query, 'seq', axis=0, tiled=True)]
    ppermute x0 -> x15, starting transfers between devices: none -> 32 us  [the longest x7 31.7 us: recover_the_indices(): n_now = lax.ppermute(w1[-1], axis_name=along_axis, perm=arrivals)]
    all_gather x1 -> x0, waiting for transfers between devices: 31.1 us -> none  [local(): key_piece = lax.all_gather(keys, 'seq', axis=0, tiled=True)]
    ppermute x0 -> x15, waiting for transfers between devices: none -> 26.9 us  [the longest x8 23.1 us: recover_the_indices(): base_arr = lax.ppermute(mid_arr[-1], along_axis, line_up)]
    unnamed x4 -> x35, local copies, waits for them, and re-layouts: 0.01 us -> 19.8 us
    all_gather x1, waiting for transfers between devices: 39.3 us -> 28 us  [local(): value_piece = lax.all_gather(values, 'seq', axis=0, tiled=True)]
  transfers between devices with their start and end apart: 7 -> 21, of which waited for: 7 -> 16; matrix products, arithmetic and copies ran while one was open for 11% -> 17% of each run, Pallas kernels for 0% -> 0%
where the time goes in v1:
time: 369 us
  waiting for transfers between devices  252 us (68%)
  matrix products  36.9 us (10%)
  starting transfers between devices  32.2 us (9%)
  local copies, waits for them, and re-layouts  21 us (6%)
  other arithmetic  13.8 us (4%)
  between operations  13.6 us (4%)
    all_gather x1, waiting for transfers between devices, local(): lax.all_gather(w_out, 'seq', axis=1, tiled=True)  58.9 us
    reduce_scatter x1, waiting for transfers between devices, local(): lax.psum_scatter(partial_out.astype(jnp.bfloat16), 'head', scatter_dimens...  58.4 us
    all_gather x1, waiting for transfers between devices, local(): lax.all_gather(w_value, 'seq', axis=0, tiled=True)  40.2 us
    all_gather x1, waiting for transfers between devices, local(): lax.all_gather(w_key, 'seq', axis=0, tiled=True)  36.5 us
    ppermute x7, starting transfers between devices, recover_the_indices(): n_now = lax.ppermute(w1[-1], axis_name=along_axis, perm=arrivals)  31.7 us
    all_gather x1, waiting for transfers between devices, local(): value_piece = lax.all_gather(values, 'seq', axis=0, tiled=True)  28 us
    ppermute x8, waiting for transfers between devices, recover_the_indices(): base_arr = lax.ppermute(mid_arr[-1], along_axis, line_up)  23.1 us
    unnamed x35, local copies, waits for them, and re-layouts  19.8 us
  transfers between devices with their start and end apart: 21, of which 16 were waited for; matrix products, arithmetic and copies ran while one was open for 17% of the time, Pallas kernels for 0%

profile of v1, /device:TPU:0, one launch (start us, length us, event | category | flops | bytes accessed | tf_op | source)
XLA Modules:
  0.0 369.1 jit_solution(4852879712023571415)
XLA Ops:
  10.2 3.4 fusion.13
  13.5 40.2 %all-gather.10.cloned.1.call-done = bf16[8192,128]{1,0:T(8,128)(2,1)} async-done(((bf16[512,128]{1,0:T(8,128)(2,1)}), bf16[8192,128]{1,0:T(8,128)(2,1)}) %all-gather.10.cloned.1.call-update) | async-done | bytes 2097168 | tf_op jit(solution)/shard_map/all_gather | solution.py:69
  53.7 5.2 %fusion.17 = bf16[288,128]{1,0:T(8,128)(2,1)} fusion(bf16[8192,128]{1,0:T(8,128)(2,1)} %all-gather.10.cloned.1.call-done, f32[128]{0:T(128)S(1)} %convert_element_type.57, bf16[288,8192]{1,0:T(8,128)(2,1)} %param.11, f32[8192]{0:T(1024)S(1)} %convert_element_type.51, f32[288]{0:T(512)S(1)} %add_rsqrt_fusion), kind=kOutput, calls=%fused_computation.27 | convolution fusion | flops 613490688 | bytes 6923904 | tf_op jit(solution)/shard_map/dot_general | solution.py:67
  59.6 36.5 %all-gather.6.cloned.1.call-done = bf16[8192,128]{1,0:T(8,128)(2,1)} async-done(((bf16[512,128]{1,0:T(8,128)(2,1)}), bf16[8192,128]{1,0:T(8,128)(2,1)}) %all-gather.6.cloned.1.call-update) | async-done | bytes 2097168 | tf_op jit(solution)/shard_map/all_gather | solution.py:65
  96.1 4.6 %fusion.16 = f32[288,1,128]{2,0,1:T(8,128)S(1)} fusion(bf16[8192,128]{1,0:T(8,128)(2,1)} %all-gather.6.cloned.1.call-done, f32[128]{0:T(128)S(1)} %convert_element_type.53, bf16[288,8192]{1,0:T(8,128)(2,1)} %param.11, f32[8192]{0:T(1024)S(1)} %convert_element_type.51, f32[288]{0:T(512)S(1)} %add_rsqrt_fusion), kind=kOutput, calls=%fused_computation.26 | convolution fusion | flops 613453824 | bytes 6997632 | tf_op jit(solution)/shard_map/dot_general | solution.py:64
  101.7 6.3 %collective-permute-done = bf16[288,128]{1,0:T(8,128)(2,1)S(1)} collective-permute-done((bf16[288,128]{1,0:T(8,128)(2,1)S(1)}, bf16[288,128]{1,0:T(8,128)(2,1)S(1)}, u32[]{:S(2)}, u32[]{:S(2)}) %collective-permute-start) | collective-permute-done | bytes 73760 | tf_op jit(solution)/shard_map/ppermute | solution.py:25
  107.9 4.4 %collective-permute-start.8 = (bf16[288,128]{1,0:T(8,128)(2,1)S(1)}, bf16[288,128]{1,0:T(8,128)(2,1)S(1)}, u32[]{:S(2)}, u32[]{:S(2)}) collective-permute-start(bf16[288,128]{1,0:T(8,128)(2,1)S(1)} %maximum_bitcast_fusion.1), channel_id=1, source_target_pairs={{0,30},{2,0},{4,2},{6,4},{8,6},{10,8},{12,10},{14,12},{16,14},{18,... | collective-permute-start | bytes 221192 | tf_op jit(solution)/shard_map/ppermute | solution.py:29
  112.4 3.7 %collective-permute-done.1 = bf16[288,128]{1,0:T(8,128)(2,1)S(1)} collective-permute-done((bf16[288,128]{1,0:T(8,128)(2,1)S(1)}, bf16[288,128]{1,0:T(8,128)(2,1)S(1)}, u32[]{:S(2)}, u32[]{:S(2)}) %collective-permute-start.1) | collective-permute-done | bytes 73760 | tf_op jit(solution)/shard_map/ppermute | solution.py:25
  116.1 4.4 %collective-permute-start.9 = (bf16[288,128]{1,0:T(8,128)(2,1)S(1)}, bf16[288,128]{1,0:T(8,128)(2,1)S(1)}, u32[]{:S(2)}, u32[]{:S(2)}) collective-permute-start(bf16[288,128]{1,0:T(8,128)(2,1)S(1)} %collective-permute-done.8), channel_id=1, source_target_pairs={{0,30},{2,0},{4,2},{6,4},{8,6},{10,8},{12,10},{14,12},{16,14},{18,... | collective-permute-start | bytes 221192 | tf_op jit(solution)/shard_map/ppermute | solution.py:29
  120.6 3.7 %collective-permute-done.2 = bf16[288,128]{1,0:T(8,128)(2,1)S(1)} collective-permute-done((bf16[288,128]{1,0:T(8,128)(2,1)S(1)}, bf16[288,128]{1,0:T(8,128)(2,1)S(1)}, u32[]{:S(2)}, u32[]{:S(2)}) %collective-permute-start.2) | collective-permute-done | bytes 73760 | tf_op jit(solution)/shard_map/ppermute | solution.py:25
  124.3 4.4 %collective-permute-start.10 = (bf16[288,128]{1,0:T(8,128)(2,1)S(1)}, bf16[288,128]{1,0:T(8,128)(2,1)S(1)}, u32[]{:S(2)}, u32[]{:S(2)}) collective-permute-start(bf16[288,128]{1,0:T(8,128)(2,1)S(1)} %collective-permute-done.9), channel_id=1, source_target_pairs={{0,30},{2,0},{4,2},{6,4},{8,6},{10,8},{12,10},{14,12},{16,14},{18,... | collective-permute-start | bytes 221192 | tf_op jit(solution)/shard_map/ppermute | solution.py:29
  130.8 4.5 %collective-permute-start.11 = (bf16[288,128]{1,0:T(8,128)(2,1)S(1)}, bf16[288,128]{1,0:T(8,128)(2,1)S(1)}, u32[]{:S(2)}, u32[]{:S(2)}) collective-permute-start(bf16[288,128]{1,0:T(8,128)(2,1)S(1)} %collective-permute-done.10), channel_id=1, source_target_pairs={{0,30},{2,0},{4,2},{6,4},{8,6},{10,8},{12,10},{14,12},{16,14},{18,... | collective-permute-start | bytes 221192 | tf_op jit(solution)/shard_map/ppermute | solution.py:29
  138.9 4.6 %collective-permute-start.12 = (bf16[288,128]{1,0:T(8,128)(2,1)S(1)}, bf16[288,128]{1,0:T(8,128)(2,1)S(1)}, u32[]{:S(2)}, u32[]{:S(2)}) collective-permute-start(bf16[288,128]{1,0:T(8,128)(2,1)S(1)} %collective-permute-done.11), channel_id=1, source_target_pairs={{0,30},{2,0},{4,2},{6,4},{8,6},{10,8},{12,10},{14,12},{16,14},{18,... | collective-permute-start | bytes 221192 | tf_op jit(solution)/shard_map/ppermute | solution.py:29
  147.1 4.6 %collective-permute-start.13 = (bf16[288,128]{1,0:T(8,128)(2,1)S(1)}, bf16[288,128]{1,0:T(8,128)(2,1)S(1)}, u32[]{:S(2)}, u32[]{:S(2)}) collective-permute-start(bf16[288,128]{1,0:T(8,128)(2,1)S(1)} %collective-permute-done.12), channel_id=1, source_target_pairs={{0,30},{2,0},{4,2},{6,4},{8,6},{10,8},{12,10},{14,12},{16,14},{18,... | collective-permute-start | bytes 221192 | tf_op jit(solution)/shard_map/ppermute | solution.py:29
  155.1 4.6 %collective-permute-start.14 = (bf16[288,128]{1,0:T(8,128)(2,1)S(1)}, bf16[288,128]{1,0:T(8,128)(2,1)S(1)}, u32[]{:S(2)}, u32[]{:S(2)}) collective-permute-start(bf16[288,128]{1,0:T(8,128)(2,1)S(1)} %collective-permute-done.13), channel_id=1, source_target_pairs={{0,30},{2,0},{4,2},{6,4},{8,6},{10,8},{12,10},{14,12},{16,14},{18,... | collective-permute-start | bytes 221192 | tf_op jit(solution)/shard_map/ppermute | solution.py:29
  181.4 7.0 %convolution_add_fusion = f32[288,512]{1,0:T(8,128)S(1)} fusion(bf16[8192,512]{1,0:T(8,128)(2,1)} %all-gather.8.cloned.1.call-done, f32[512]{0:T(512)S(1)} %convert_element_type.56, bf16[288,8192]{1,0:T(8,128)(2,1)} %param.11, f32[8192]{0:T(1024)S(1)} %convert_element_type.51, f32[288]{0:T(512)S(1)} %add_rsqrt_fusion), kind=kOutput, calls=%fused_computation.23 | convolution fusion | flops 2425503744 | bytes 13732992 | tf_op jit(solution)/shard_map/dot_general | solution.py:59
  189.4 28.0 %all-gather.12.cloned.1.call-done = bf16[4608,128]{1,0:T(8,128)(2,1)} async-done(((bf16[288,128]{1,0:T(8,128)(2,1)}), bf16[4608,128]{1,0:T(8,128)(2,1)}) %all-gather.12.cloned.1.call-update) | async-done | bytes 1179664 | tf_op jit(solution)/shard_map/all_gather | solution.py:90
  217.4 19.7 %conditional.1 = (f32[4,288]{1,0:T(4,128)S(1)}, f32[4,288,128]{2,1,0:T(8,128)S(1)}) conditional(s32[]{:T(128)} %convert_element_type.49, () %tuple.23, (s32[]{:T(128)}, s32[288]{0:T(512)S(1)}, s32[]{:T(128)}, bf16[9216,128]{1,0:T(8,128)(2,1)}, bf16[4,288,128]{2,1,0:T(8,128)(2,1)S(1)}, /*index=5*/bf16[4608,128]{1,0:T(8,128)(2,1)}) %tuple.24), branch_computations={%region_1.2_spmd, %region_2.5_spmd} | conditional | flops 2777627648 | bytes 72284696 | solution.py:115
  218.1 5.7 %fusion.2 = (f32[4,288]{1,0:T(4,128)S(1)}, f32[4608,4,288]{0,2,1:T(8,128)S(1)}) fusion(pred[288,4608]{1,0:T(8,128)(4,1)S(1)} %iota_compare_fusion, bf16[4,288,128]{2,1,0:T(8,128)(2,1)S(1)} %get-tuple-element.115, bf16[9216,128]{1,0:T(8,128)(2,1)} %get-tuple-element.113, s32[]{:T(128)S(6)} %select_n.25), kind=kOutput, calls=%fused_computation.4 | convolution fusion | flops 1374878592 | bytes 24039940 | tf_op jit(solution)/shard_map/cond/branch_1_fun/hqd,kd->hqk/dot_general | solution.py:95
  223.9 6.6 %fusion.3 = f32[4,288,128]{2,1,0:T(8,128)S(1)} fusion(f32[4608,4,288]{0,2,1:T(8,128)S(1)} %get-tuple-element.122, f32[4,288]{1,0:T(4,128)S(1)} %broadcast_maximum_fusion, pred[288,4608]{1,0:T(8,128)(4,1)S(1)} %iota_compare_fusion, bf16[4608,128]{1,0:T(8,128)(2,1)} %get-tuple-element.116), kind=kOutput, calls=%fused_computation.5 | convolution fusion | flops 1380188160 | bytes 24334848 | tf_op jit(solution)/shard_map/cond/branch_1_fun/hqk,kd->hqd/dot_general | solution.py:104
  230.5 6.6 %fusion.1 = f32[4,288]{1,0:T(4,128)S(1)} fusion(f32[4608,4,288]{0,2,1:T(8,128)S(1)} %get-tuple-element.122, f32[4,288]{1,0:T(4,128)S(1)} %broadcast_maximum_fusion, pred[288,4608]{1,0:T(8,128)(4,1)S(1)} %iota_compare_fusion), kind=kLoop, calls=%fused_computation.3 | loop fusion | flops 21232512 | bytes 22569984 | tf_op jit(solution)/shard_map/cond/branch_1_fun/reduce_sum | solution.py:103
  237.1 58.9 %all-gather.14.cloned.1.call-done = bf16[512,8192]{1,0:T(8,128)(2,1)} async-done(((bf16[512,512]{1,0:T(8,128)(2,1)}), bf16[512,8192]{1,0:T(8,128)(2,1)}) %all-gather.14.cloned.1.call-update) | async-done | bytes 8388624 | tf_op jit(solution)/shard_map/all_gather | solution.py:120
  296.0 7.8 %convolution_convert_fusion = bf16[288,8192]{1,0:T(8,128)(2,1)} fusion(bf16[512,8192]{1,0:T(8,128)(2,1)} %all-gather.14.cloned.1.call-done, f32[4,288,128]{2,1,0:T(8,128)S(1)} %get-tuple-element.119, f32[4,288]{1,0:T(4,128)S(1)} %get-tuple-element.120), kind=kOutput, calls=%fused_computation.19 | convolution fusion | flops 2418573312 | bytes 13701632 | tf_op jit(solution)/shard_map/dot_general | solution.py:118
  303.8 58.4 %reduce-scatter.2.cloned.1.call-done = bf16[144,8192]{1,0:T(8,128)(2,1)} async-done(((bf16[288,8192]{1,0:T(8,128)(2,1)}), bf16[144,8192]{1,0:T(8,128)(2,1)}) %reduce-scatter.2.cloned.1.call-update) | async-done | bytes 2359312 | tf_op jit(solution)/shard_map/reduce_scatter | solution.py:123
  (87 shorter events, 41.2 us)
Async XLA Ops:
  6.5 47.2 %all-gather.10.cloned.1.call-start = ((), (), s32[]{:S(2)}) async-start(), calls=%async_computation.3 | async-start | bytes 2228224 | tf_op jit(solution)/shard_map/all_gather | solution.py:69
  7.3 88.8 %all-gather.6.cloned.1.call-start = ((), (), s32[]{:S(2)}) async-start(), calls=%async_computation.1 | async-start | bytes 2228224 | tf_op jit(solution)/shard_map/all_gather | solution.py:65
  8.0 173.4 %all-gather.8.cloned.1.call-start = ((), (), s32[]{:S(2)}) async-start(), calls=%async_computation.2 | async-start | bytes 8912896 | tf_op jit(solution)/shard_map/all_gather | solution.py:61
  8.7 208.6 %all-gather.12.cloned.1.call-start = ((), (), s32[]{:S(2)}) async-start(), calls=%async_computation.4 | async-start | bytes 1253376 | tf_op jit(solution)/shard_map/all_gather | solution.py:90
  13.5 46.0 %copy-start.1 = (bf16[128]{0:T(256)(128)(2,1)S(1)}, bf16[128]{0:T(256)(128)(2,1)}, u32[]{:S(2)}) copy-start(bf16[128]{0:T(256)(128)(2,1)} %param.17) | copy-start | bytes 772
  58.9 237.1 %all-gather.14.cloned.1.call-start = ((), (), s32[]{:S(2)}) async-start(), calls=%async_computation.5 | async-start | bytes 8912896 | tf_op jit(solution)/shard_map/all_gather | solution.py:120
  59.5 302.8 %reduce-scatter.2.cloned.1.call-start = ((), (), s32[]{:S(2)}) async-start(), calls=%async_computation.6 | async-start | bytes 7077888 | tf_op jit(solution)/shard_map/reduce_scatter | solution.py:123
  59.6 94.8 %copy-start = (bf16[512]{0:T(512)(128)(2,1)S(1)}, bf16[512]{0:T(512)(128)(2,1)}, u32[]{:S(2)}) copy-start(bf16[512]{0:T(512)(128)(2,1)} %param.16) | copy-start | bytes 3076
  101.4 6.5 %collective-permute-start = (bf16[288,128]{1,0:T(8,128)(2,1)S(1)}, bf16[288,128]{1,0:T(8,128)(2,1)S(1)}, u32[]{:S(2)}, u32[]{:S(2)}) collective-permute-start(bf16[288,128]{1,0:T(8,128)(2,1)S(1)} %maximum_bitcast_fusion.1), channel_id=1, source_target_pairs={{0,2},{2,4},{4,6},{6,8},{8,10},{10,12},{12,14},{14,16},{16,18},{18... | collective-permute-start | bytes 221192 | tf_op jit(solution)/shard_map/ppermute | solution.py:25
  107.9 8.2 %collective-permute-start.1 = (bf16[288,128]{1,0:T(8,128)(2,1)S(1)}, bf16[288,128]{1,0:T(8,128)(2,1)S(1)}, u32[]{:S(2)}, u32[]{:S(2)}) collective-permute-start(bf16[288,128]{1,0:T(8,128)(2,1)S(1)} %collective-permute-done), channel_id=1, source_target_pairs={{0,2},{2,4},{4,6},{6,8},{8,10},{10,12},{12,14},{14,16},{16,18},{18... | collective-permute-start | bytes 221192 | tf_op jit(solution)/shard_map/ppermute | solution.py:25
  107.9 8.2 %collective-permute-start.8 = (bf16[288,128]{1,0:T(8,128)(2,1)S(1)}, bf16[288,128]{1,0:T(8,128)(2,1)S(1)}, u32[]{:S(2)}, u32[]{:S(2)}) collective-permute-start(bf16[288,128]{1,0:T(8,128)(2,1)S(1)} %maximum_bitcast_fusion.1), channel_id=1, source_target_pairs={{0,30},{2,0},{4,2},{6,4},{8,6},{10,8},{12,10},{14,12},{16,14},{18,... | collective-permute-start | bytes 221192 | tf_op jit(solution)/shard_map/ppermute | solution.py:29
  116.1 8.2 %collective-permute-start.2 = (bf16[288,128]{1,0:T(8,128)(2,1)S(1)}, bf16[288,128]{1,0:T(8,128)(2,1)S(1)}, u32[]{:S(2)}, u32[]{:S(2)}) collective-permute-start(bf16[288,128]{1,0:T(8,128)(2,1)S(1)} %collective-permute-done.1), channel_id=1, source_target_pairs={{0,2},{2,4},{4,6},{6,8},{8,10},{10,12},{12,14},{14,16},{16,18},{18... | collective-permute-start | bytes 221192 | tf_op jit(solution)/shard_map/ppermute | solution.py:25
  116.1 8.2 %collective-permute-start.9 = (bf16[288,128]{1,0:T(8,128)(2,1)S(1)}, bf16[288,128]{1,0:T(8,128)(2,1)S(1)}, u32[]{:S(2)}, u32[]{:S(2)}) collective-permute-start(bf16[288,128]{1,0:T(8,128)(2,1)S(1)} %collective-permute-done.8), channel_id=1, source_target_pairs={{0,30},{2,0},{4,2},{6,4},{8,6},{10,8},{12,10},{14,12},{16,14},{18,... | collective-permute-start | bytes 221192 | tf_op jit(solution)/shard_map/ppermute | solution.py:29
  124.3 6.5 %collective-permute-start.3 = (bf16[288,128]{1,0:T(8,128)(2,1)S(1)}, bf16[288,128]{1,0:T(8,128)(2,1)S(1)}, u32[]{:S(2)}, u32[]{:S(2)}) collective-permute-start(bf16[288,128]{1,0:T(8,128)(2,1)S(1)} %collective-permute-done.2), channel_id=1, source_target_pairs={{0,2},{2,4},{4,6},{6,8},{8,10},{10,12},{12,14},{14,16},{16,18},{18... | collective-permute-start | bytes 221192 | tf_op jit(solution)/shard_map/ppermute | solution.py:25
  124.3 6.5 %collective-permute-start.10 = (bf16[288,128]{1,0:T(8,128)(2,1)S(1)}, bf16[288,128]{1,0:T(8,128)(2,1)S(1)}, u32[]{:S(2)}, u32[]{:S(2)}) collective-permute-start(bf16[288,128]{1,0:T(8,128)(2,1)S(1)} %collective-permute-done.9), channel_id=1, source_target_pairs={{0,30},{2,0},{4,2},{6,4},{8,6},{10,8},{12,10},{14,12},{16,14},{18,... | collective-permute-start | bytes 221192 | tf_op jit(solution)/shard_map/ppermute | solution.py:29
  130.8 6.6 %collective-permute-start.4 = (bf16[288,128]{1,0:T(8,128)(2,1)S(1)}, bf16[288,128]{1,0:T(8,128)(2,1)S(1)}, u32[]{:S(2)}, u32[]{:S(2)}) collective-permute-start(bf16[288,128]{1,0:T(8,128)(2,1)S(1)} %collective-permute-done.3), channel_id=1, source_target_pairs={{0,2},{2,4},{4,6},{6,8},{8,10},{10,12},{12,14},{14,16},{16,18},{18... | collective-permute-start | bytes 221192 | tf_op jit(solution)/shard_map/ppermute | solution.py:25
  130.8 8.2 %collective-permute-start.11 = (bf16[288,128]{1,0:T(8,128)(2,1)S(1)}, bf16[288,128]{1,0:T(8,128)(2,1)S(1)}, u32[]{:S(2)}, u32[]{:S(2)}) collective-permute-start(bf16[288,128]{1,0:T(8,128)(2,1)S(1)} %collective-permute-done.10), channel_id=1, source_target_pairs={{0,30},{2,0},{4,2},{6,4},{8,6},{10,8},{12,10},{14,12},{16,14},{18,... | collective-permute-start | bytes 221192 | tf_op jit(solution)/shard_map/ppermute | solution.py:29
  137.4 8.2 %collective-permute-start.5 = (bf16[288,128]{1,0:T(8,128)(2,1)S(1)}, bf16[288,128]{1,0:T(8,128)(2,1)S(1)}, u32[]{:S(2)}, u32[]{:S(2)}) collective-permute-start(bf16[288,128]{1,0:T(8,128)(2,1)S(1)} %collective-permute-done.4), channel_id=1, source_target_pairs={{0,2},{2,4},{4,6},{6,8},{8,10},{10,12},{12,14},{14,16},{16,18},{18... | collective-permute-start | bytes 221192 | tf_op jit(solution)/shard_map/ppermute | solution.py:25
  138.9 8.2 %collective-permute-start.12 = (bf16[288,128]{1,0:T(8,128)(2,1)S(1)}, bf16[288,128]{1,0:T(8,128)(2,1)S(1)}, u32[]{:S(2)}, u32[]{:S(2)}) collective-permute-start(bf16[288,128]{1,0:T(8,128)(2,1)S(1)} %collective-permute-done.11), channel_id=1, source_target_pairs={{0,30},{2,0},{4,2},{6,4},{8,6},{10,8},{12,10},{14,12},{16,14},{18,... | collective-permute-start | bytes 221192 | tf_op jit(solution)/shard_map/ppermute | solution.py:29
  145.6 8.2 %collective-permute-start.6 = (bf16[288,128]{1,0:T(8,128)(2,1)S(1)}, bf16[288,128]{1,0:T(8,128)(2,1)S(1)}, u32[]{:S(2)}, u32[]{:S(2)}) collective-permute-start(bf16[288,128]{1,0:T(8,128)(2,1)S(1)} %collective-permute-done.5), channel_id=1, source_target_pairs={{0,2},{2,4},{4,6},{6,8},{8,10},{10,12},{12,14},{14,16},{16,18},{18... | collective-permute-start | bytes 221192 | tf_op jit(solution)/shard_map/ppermute | solution.py:25
  147.1 7.9 %collective-permute-start.13 = (bf16[288,128]{1,0:T(8,128)(2,1)S(1)}, bf16[288,128]{1,0:T(8,128)(2,1)S(1)}, u32[]{:S(2)}, u32[]{:S(2)}) collective-permute-start(bf16[288,128]{1,0:T(8,128)(2,1)S(1)} %collective-permute-done.12), channel_id=1, source_target_pairs={{0,30},{2,0},{4,2},{6,4},{8,6},{10,8},{12,10},{14,12},{16,14},{18,... | collective-permute-start | bytes 221192 | tf_op jit(solution)/shard_map/ppermute | solution.py:29
  153.8 7.2 %collective-permute-start.7 = (bf16[288,128]{1,0:T(8,128)(2,1)S(1)}, bf16[288,128]{1,0:T(8,128)(2,1)S(1)}, u32[]{:S(2)}, u32[]{:S(2)}) collective-permute-start(bf16[288,128]{1,0:T(8,128)(2,1)S(1)} %collective-permute-done.6), channel_id=1, source_target_pairs={{0,2},{2,4},{4,6},{6,8},{8,10},{10,12},{12,14},{14,16},{16,18},{18... | collective-permute-start | bytes 221192 | tf_op jit(solution)/shard_map/ppermute | solution.py:25
  155.1 15.5 %collective-permute-start.14 = (bf16[288,128]{1,0:T(8,128)(2,1)S(1)}, bf16[288,128]{1,0:T(8,128)(2,1)S(1)}, u32[]{:S(2)}, u32[]{:S(2)}) collective-permute-start(bf16[288,128]{1,0:T(8,128)(2,1)S(1)} %collective-permute-done.13), channel_id=1, source_target_pairs={{0,30},{2,0},{4,2},{6,4},{8,6},{10,8},{12,10},{14,12},{16,14},{18,... | collective-permute-start | bytes 221192 | tf_op jit(solution)/shard_map/ppermute | solution.py:29
Sparse Core Ops, SparseCore 0:
  9.5 44.1 all-gather.9
  55.9 40.1 all-gather.5
  98.2 79.0 all-gather.7
  179.4 37.9 all-gather.11
  219.4 76.5 all-gather.13
  304.0 58.2 reduce-scatter.1
